TPU v7x, 32 devices: a whole 2x2x4 slice. The times are simulated.
32 devices in a mesh: group: 8 (over z, y), tok: 4 (over x, core).
Axes of the slice: x: 2, y: 2, z: 4, core: 2. Of those that a mesh axis runs over, the one named last changes fastest.
Arguments:
- tokens: bfloat16 [16384, 2048], P(('group', 'tok')), may hold values from -94 to 94
- learning_rates: float32 [2, 16384], P(None, 'group'), may hold values from 0.1 to 1
- channel_gains: float32 [2, 5, 2048], P(None, None, 'tok'), may hold values from 0.3 to 3
- fast_init: float32 [2, 3, 16, 128, 128], P(None, None, 'tok'), may hold values from -0.5 to 0.5
- step_size: float32 [2, 16], P(None, 'tok'), may hold values from 0.05 to 1
- update_table: int32 [2, 8], replicated, may hold values 0 or 1
Outputs:
- mixed: bfloat16 [16384, 2048], P(('group', 'tok'))
All inputs are finite; a program needn't handle non-finite values.
Results may differ from a plain program's by a relative error of at most 0.033.
Values may be sent and summed in bfloat16 or wider, within the bound.
A program may use at most 64 MiB of HBM per device.

v0:
```python
import jax
import jax.numpy as jnp
from jax import lax
from jax.sharding import PartitionSpec as P

NS_STEPS = 5
MUON_A = 3.4445
MUON_B = -4.775
MUON_C = 2.0315
EPSILON = 1e-06


def passed_along(value, axis, by):
    size = lax.axis_size(axis)
    pairs = [(i, i + by) for i in range(size) if 0 <= i + by < size]
    return lax.ppermute(value, axis, pairs)


def orthogonalize(gradient):
    scaling = lax.rsqrt(jnp.sum(gradient * gradient, axis=(-2, -1), keepdims=True) + EPSILON)
    current = gradient * scaling
    for repeat in range(NS_STEPS):
        square = jnp.einsum("...ij,...kj->...ik", current, current, precision=lax.Precision.HIGHEST)
        polynom = MUON_B * square + MUON_C * jnp.einsum(
            "...ij,...jk->...ik", square, square, precision=lax.Precision.HIGHEST
        )
        current = MUON_A * current + jnp.einsum(
            "...ij,...jk->...ik", polynom, current, precision=lax.Precision.HIGHEST
        )
    return current


def layer_group(stream, entering, gain_rows, rates_row, steps_row, update_flag, inverse):
    row_count, channel_count = stream.shape
    heads_n = entering.shape[1]
    head_dim = entering.shape[2]
    normed = stream.astype(jnp.float32) * inverse[:, None] * gain_rows[0]
    queries = (normed * gain_rows[1]).astype(jnp.bfloat16).reshape(row_count, heads_n, head_dim)
    keys_in = (normed * gain_rows[2]).astype(jnp.bfloat16).reshape(row_count, heads_n, head_dim)
    values_in = (normed * gain_rows[3]).astype(jnp.bfloat16).reshape(row_count, heads_n, head_dim)
    rounded = entering.astype(jnp.bfloat16)
    gate_q = jnp.einsum("thi,hij->thj", queries, rounded[0], preferred_element_type=jnp.float32)
    up_q = jnp.einsum("thi,hij->thj", queries, rounded[1], preferred_element_type=jnp.float32)
    hidden_q = (jax.nn.silu(gate_q) * up_q).astype(jnp.bfloat16)
    output = jnp.einsum(
        "thj,hjk->thk", hidden_q, rounded[2], preferred_element_type=jnp.float32
    ).reshape(row_count, channel_count)
    mixed_rows = (stream.astype(jnp.float32) + gain_rows[4] * output).astype(jnp.bfloat16)
    gate_k = jnp.einsum("thi,hij->thj", keys_in, rounded[0], preferred_element_type=jnp.float32)
    up_k = jnp.einsum("thi,hij->thj", keys_in, rounded[1], preferred_element_type=jnp.float32)
    sigmoid_k = jax.nn.sigmoid(gate_k)
    active_k = gate_k * sigmoid_k
    hidden_k = (active_k * up_k).astype(jnp.bfloat16)
    targets = (rates_row[:, None, None] * values_in.astype(jnp.float32)).astype(jnp.bfloat16)
    back_hidden = jnp.einsum(
        "thk,hjk->thj", targets, rounded[2], preferred_element_type=jnp.float32
    )
    back_up = (back_hidden * active_k).astype(jnp.bfloat16)
    back_gate = (back_hidden * up_k * sigmoid_k * (1.0 + gate_k * (1.0 - sigmoid_k))).astype(
        jnp.bfloat16
    )
    grad_gate = jnp.einsum("thi,thj->hij", keys_in, back_gate, preferred_element_type=jnp.float32)
    grad_up = jnp.einsum("thi,thj->hij", keys_in, back_up, preferred_element_type=jnp.float32)
    grad_down = jnp.einsum("thj,thk->hjk", hidden_k, targets, preferred_element_type=jnp.float32)
    direction = orthogonalize(jnp.stack([grad_gate, grad_up, grad_down]))
    moved_state = entering + (update_flag * steps_row)[None, :, None, None] * direction
    norm_before = jnp.sqrt(jnp.sum(entering * entering, axis=2, keepdims=True) + EPSILON)
    norm_after = jnp.sqrt(jnp.sum(moved_state * moved_state, axis=2, keepdims=True) + EPSILON)
    return (mixed_rows, moved_state * (norm_before / norm_after))


def pass_on(outgoing):
    return passed_along(outgoing, "group", 1)


def body(tokens, learning_rates, channel_gains, fast_init, step_size, update_table):
    start_stream = lax.all_to_all(tokens, "tok", split_axis=1, concat_axis=0, tiled=True)
    group_count = lax.axis_size("group")
    group_index = lax.axis_index("group")
    width_all = start_stream.shape[1] * lax.axis_size("tok")
    layer_count = fast_init.shape[0]
    zero_state = jnp.zeros(fast_init.shape[1:], jnp.float32)

    def tick_work(stream, outgoing, layer_now, active, inverse):
        received = pass_on(outgoing)
        initial = lax.dynamic_index_in_dim(fast_init, layer_now, 0, keepdims=False)
        entering = jnp.where(group_index == 0, initial, received)
        gain_rows = lax.dynamic_index_in_dim(channel_gains, layer_now, 0, keepdims=False)
        rates_row = lax.dynamic_index_in_dim(learning_rates, layer_now, 0, keepdims=False)
        steps_row = lax.dynamic_index_in_dim(step_size, layer_now, 0, keepdims=False)
        table_cell = lax.dynamic_slice(
            update_table, (jnp.asarray(layer_now, jnp.int32), group_index), (1, 1)
        )
        update_flag = table_cell[0, 0].astype(jnp.float32)

        def working(operands):
            return layer_group(
                operands[0], operands[1], gain_rows, rates_row, steps_row, update_flag, inverse
            )

        def resting(operands):
            return (operands[0], operands[2])

        return lax.cond(active, working, resting, (stream, entering, outgoing))

    def one_tick(tick_index, loop_state):
        stream, outgoing = loop_state
        layer_raw = tick_index - group_index
        active = (layer_raw >= 0) & (layer_raw < layer_count)
        layer_now = jnp.clip(layer_raw, 0, layer_count - 1)
        widened = stream.astype(jnp.float32)
        totals = lax.psum(jnp.sum(widened * widened, axis=1), "tok")
        inverse = lax.rsqrt(totals / width_all + EPSILON)
        return tick_work(stream, outgoing, layer_now, active, inverse)

    final_stream, last_state = lax.fori_loop(
        0, layer_count + group_count - 1, one_tick, (start_stream, zero_state)
    )
    return lax.all_to_all(final_stream, "tok", split_axis=0, concat_axis=1, tiled=True)


def solution(mesh):
    in_specs = (
        P(("group", "tok"), None),
        P(None, "group"),
        P(None, None, "tok"),
        P(None, None, "tok", None, None),
        P(None, "tok"),
        P(),
    )
    out_specs = P(("group", "tok"), None)
    return jax.shard_map(body, mesh=mesh, in_specs=in_specs, out_specs=out_specs, check_vma=False)
```

profile of v0, /device:TPU:28, one launch (start us, length us, event | category | flops | bytes accessed | tf_op | source)
XLA Modules:
  0.0 798.3 jit_solution(697076841951351439)
XLA Ops:
  0.0 3.9 copy.32
  3.9 3.6 all-to-all-start
  7.6 25.6 %all-to-all-done = bf16[512,4,512]{0,2,1:T(8,128)(2,1)S(1)} async-done(((bf16[512,4,512]{0,2,1:T(8,128)(2,1)}), bf16[512,4,512]{0,2,1:T(8,128)(2,1)S(1)}, u32[]{:S(2)}, u32[]{:S(2)}) %all-to-all-start) | async-done | bytes 2097184 | tf_op jit(solution)/shard_map/all_to_all | solution.py:77
  33.2 2.4 copy.33
  35.5 2.9 copy.34
  39.4 719.4 %while.17 = (s32[]{:T(128)}, bf16[2048,512]{0,1:T(8,128)(2,1)S(1)}, f32[3,4,128,128]{3,2,1,0:T(8,128)}, s32[]{:T(128)}, f32[2,5,512]{2,1,0:T(8,128)S(1)}, /*inde...) while((s32[]{:T(128)}, bf16[2048,512]{0,1:T(8,128)(2,1)S(1)}, ...), condition=%wide.region_8.9_spmd, body=%wide.region_0.8_spmd.sunk | while | flops 7005345280 | bytes 224676816 | solution.py:116
  39.4 1.3 collective-permute-start
  41.2 6.1 psum.14
  47.3 13.3 %collective-permute-done = f32[3,4,128,128]{3,2,1,0:T(8,128)S(1)} collective-permute-done((f32[3,4,128,128]{3,2,1,0:T(8,128)}, f32[3,4,128,128]{3,2,1,0:T(8,128)S(1)}, u32[]{:S(2)}, u32[]{:S(2)}) %collective-permute-start) | collective-permute-done | bytes 786464 | tf_op jit(solution)/shard_map/while/body/eval_jaxpr/ppermute | solution.py:16
  62.3 6.1 psum.14
  68.3 12.4 %collective-permute-done = f32[3,4,128,128]{3,2,1,0:T(8,128)S(1)} collective-permute-done((f32[3,4,128,128]{3,2,1,0:T(8,128)}, f32[3,4,128,128]{3,2,1,0:T(8,128)S(1)}, u32[]{:S(2)}, u32[]{:S(2)}) %collective-permute-start) | collective-permute-done | bytes 786464 | tf_op jit(solution)/shard_map/while/body/eval_jaxpr/ppermute | solution.py:16
  82.5 5.8 psum.14
  88.3 12.4 %collective-permute-done = f32[3,4,128,128]{3,2,1,0:T(8,128)S(1)} collective-permute-done((f32[3,4,128,128]{3,2,1,0:T(8,128)}, f32[3,4,128,128]{3,2,1,0:T(8,128)S(1)}, u32[]{:S(2)}, u32[]{:S(2)}) %collective-permute-start) | collective-permute-done | bytes 786464 | tf_op jit(solution)/shard_map/while/body/eval_jaxpr/ppermute | solution.py:16
  102.4 5.8 psum.14
  108.2 11.9 %collective-permute-done = f32[3,4,128,128]{3,2,1,0:T(8,128)S(1)} collective-permute-done((f32[3,4,128,128]{3,2,1,0:T(8,128)}, f32[3,4,128,128]{3,2,1,0:T(8,128)S(1)}, u32[]{:S(2)}, u32[]{:S(2)}) %collective-permute-start) | collective-permute-done | bytes 786464 | tf_op jit(solution)/shard_map/while/body/eval_jaxpr/ppermute | solution.py:16
  121.9 5.8 psum.14
  127.6 11.0 %collective-permute-done = f32[3,4,128,128]{3,2,1,0:T(8,128)S(1)} collective-permute-done((f32[3,4,128,128]{3,2,1,0:T(8,128)}, f32[3,4,128,128]{3,2,1,0:T(8,128)S(1)}, u32[]{:S(2)}, u32[]{:S(2)}) %collective-permute-start) | collective-permute-done | bytes 786464 | tf_op jit(solution)/shard_map/while/body/eval_jaxpr/ppermute | solution.py:16
  140.4 5.8 psum.14
  146.3 10.1 %collective-permute-done = f32[3,4,128,128]{3,2,1,0:T(8,128)S(1)} collective-permute-done((f32[3,4,128,128]{3,2,1,0:T(8,128)}, f32[3,4,128,128]{3,2,1,0:T(8,128)S(1)}, u32[]{:S(2)}, u32[]{:S(2)}) %collective-permute-start) | collective-permute-done | bytes 786464 | tf_op jit(solution)/shard_map/while/body/eval_jaxpr/ppermute | solution.py:16
  158.1 6.2 psum.14
  164.3 8.9 %collective-permute-done = f32[3,4,128,128]{3,2,1,0:T(8,128)S(1)} collective-permute-done((f32[3,4,128,128]{3,2,1,0:T(8,128)}, f32[3,4,128,128]{3,2,1,0:T(8,128)S(1)}, u32[]{:S(2)}, u32[]{:S(2)}) %collective-permute-start) | collective-permute-done | bytes 786464 | tf_op jit(solution)/shard_map/while/body/eval_jaxpr/ppermute | solution.py:16
  173.2 1.3 collective-permute-start
  175.0 6.6 psum.14
  181.5 436.1 %collective-permute-done = f32[3,4,128,128]{3,2,1,0:T(8,128)S(1)} collective-permute-done((f32[3,4,128,128]{3,2,1,0:T(8,128)}, f32[3,4,128,128]{3,2,1,0:T(8,128)S(1)}, u32[]{:S(2)}, u32[]{:S(2)}) %collective-permute-start) | collective-permute-done | bytes 786464 | tf_op jit(solution)/shard_map/while/body/eval_jaxpr/ppermute | solution.py:16
  617.6 62.2 %conditional.2 = ((bf16[2048,512]{0,1:T(8,128)(2,1)S(1)}, f32[3,4,128,128]{3,2,1,0:T(8,128)})) conditional(s32[]{:T(128)} %convert_element_type.141, (bf16[2048,512]{0,1:T(8,128)(2,1)S(1)}, f32[3,4,128,128]{3,2,1,0:T(8,128)}) %tuple.63, (bf16[2048,512]{0,1:T(8,128)(2,1)S(1)}, s32[]{:T(128)}, f32[2,5,512]{2,1,0:T(8,128)S(1)}, f32[2048]{0:T(1024)S(1)}, ...), branch_computations={%region_3.3_spmd, %region_4.7_spmd} | conditional | flops 7002199552 | bytes 219409024 | solution.py:104
  617.6 2.6 fusion.6
  620.3 1.9 multiply_reduce_fusion.1
  622.3 2.8 fusion.50
  625.1 6.7 fusion.27
  631.8 3.3 fusion.7
  635.1 2.8 fusion.51
  637.9 2.9 fusion.49
  640.8 4.1 copy.28
  644.9 6.6 fusion.35
  654.3 1.6 fusion.38
  656.5 2.4 fusion.41
  659.0 1.9 fusion.44
  662.9 1.7 fusion.61
  666.5 1.7 fusion.62
  670.1 1.7 fusion.63
  673.8 1.8 fusion.64
  681.6 7.0 psum.14
  688.6 8.0 %collective-permute-done = f32[3,4,128,128]{3,2,1,0:T(8,128)S(1)} collective-permute-done((f32[3,4,128,128]{3,2,1,0:T(8,128)}, f32[3,4,128,128]{3,2,1,0:T(8,128)S(1)}, u32[]{:S(2)}, u32[]{:S(2)}) %collective-permute-start) | collective-permute-done | bytes 786464 | tf_op jit(solution)/shard_map/while/body/eval_jaxpr/ppermute | solution.py:16
  696.6 62.2 %conditional.2 = ((bf16[2048,512]{0,1:T(8,128)(2,1)S(1)}, f32[3,4,128,128]{3,2,1,0:T(8,128)})) conditional(s32[]{:T(128)} %convert_element_type.141, (bf16[2048,512]{0,1:T(8,128)(2,1)S(1)}, f32[3,4,128,128]{3,2,1,0:T(8,128)}) %tuple.63, (bf16[2048,512]{0,1:T(8,128)(2,1)S(1)}, s32[]{:T(128)}, f32[2,5,512]{2,1,0:T(8,128)S(1)}, f32[2048]{0:T(1024)S(1)}, ...), branch_computations={%region_3.3_spmd, %region_4.7_spmd} | conditional | flops 7002199552 | bytes 219409024 | solution.py:104
  696.7 2.6 fusion.6
  699.3 1.9 multiply_reduce_fusion.1
  701.3 2.8 fusion.50
  704.1 6.7 fusion.27
  710.8 3.3 fusion.7
  714.1 2.8 fusion.51
  716.9 2.9 fusion.49
  719.8 4.1 copy.28
  723.9 6.6 fusion.35
  733.4 1.6 fusion.38
  735.5 2.4 fusion.41
  738.1 1.9 fusion.44
  741.9 1.7 fusion.61
  745.5 1.7 fusion.62
  749.1 1.7 fusion.63
  752.8 1.8 fusion.64
  758.9 2.5 copy.36
  761.4 30.7 %all_to_all.38 = bf16[4,512,512]{2,1,0:T(8,128)(2,1)S(1)} all-to-all(bf16[4,512,512]{2,1,0:T(8,128)(2,1)} %bitcast.167), channel_id=1, replica_groups=mesh['group'=8,'tok'=4] {'tok'}, dimensions={0} | all-to-all | bytes 4194304 | tf_op jit(solution)/shard_map/all_to_all | solution.py:119
  792.1 2.4 copy.37
  794.4 3.9 copy.38
  (107 shorter events, 43.6 us)
Async XLA Ops:
  0.0 7.6 copy-start.9
  3.9 29.2 %all-to-all-start = ((bf16[512,4,512]{0,2,1:T(8,128)(2,1)}), bf16[512,4,512]{0,2,1:T(8,128)(2,1)S(1)}, u32[]{:S(2)}, u32[]{:S(2)}) async-start(bf16[512,4,512]{0,2,1:T(8,128)(2,1)} %bitcast.165), calls=%async_computation | async-start | bytes 4194304 | tf_op jit(solution)/shard_map/all_to_all | solution.py:77
  7.6 31.8 %copy-start.8 = (f32[2,2048]{1,0:T(2,128)S(1)}, f32[2,2048]{1,0:T(2,128)}, u32[]{:S(2)}) copy-start(f32[2,2048]{1,0:T(2,128)} %param.11) | copy-start | bytes 49156
  7.6 31.8 %copy-start.10 = (s32[2,8]{1,0:T(2,128)S(1)}, s32[2,8]{1,0:T(2,128)}, u32[]{:S(2)}) copy-start(s32[2,8]{1,0:T(2,128)} %param.15) | copy-start | bytes 196
  7.6 31.8 %copy-start.11 = (f32[2,4]{1,0:T(2,128)S(1)}, f32[2,4]{1,0:T(2,128)}, u32[]{:S(2)}) copy-start(f32[2,4]{1,0:T(2,128)} %param.14) | copy-start | bytes 100
  39.4 21.1 %collective-permute-start = (f32[3,4,128,128]{3,2,1,0:T(8,128)}, f32[3,4,128,128]{3,2,1,0:T(8,128)S(1)}, u32[]{:S(2)}, u32[]{:S(2)}) collective-permute-start(f32[3,4,128,128]{3,2,1,0:T(8,128)} %get-tuple-element.519), channel_id=1, source_target_pairs={{0,4},{4,8},{8,12},{12,16},{16,20},{20,24},{24,28},{1,5},{5,9},{9,... | collective-permute-start | bytes 2359304 | tf_op jit(solution)/shard_map/while/body/eval_jaxpr/ppermute | solution.py:16
  60.5 20.2 %collective-permute-start = (f32[3,4,128,128]{3,2,1,0:T(8,128)}, f32[3,4,128,128]{3,2,1,0:T(8,128)S(1)}, u32[]{:S(2)}, u32[]{:S(2)}) collective-permute-start(f32[3,4,128,128]{3,2,1,0:T(8,128)} %get-tuple-element.519), channel_id=1, source_target_pairs={{0,4},{4,8},{8,12},{12,16},{16,20},{20,24},{24,28},{1,5},{5,9},{9,... | collective-permute-start | bytes 2359304 | tf_op jit(solution)/shard_map/while/body/eval_jaxpr/ppermute | solution.py:16
  80.8 19.9 %collective-permute-start = (f32[3,4,128,128]{3,2,1,0:T(8,128)}, f32[3,4,128,128]{3,2,1,0:T(8,128)S(1)}, u32[]{:S(2)}, u32[]{:S(2)}) collective-permute-start(f32[3,4,128,128]{3,2,1,0:T(8,128)} %get-tuple-element.519), channel_id=1, source_target_pairs={{0,4},{4,8},{8,12},{12,16},{16,20},{20,24},{24,28},{1,5},{5,9},{9,... | collective-permute-start | bytes 2359304 | tf_op jit(solution)/shard_map/while/body/eval_jaxpr/ppermute | solution.py:16
  100.7 19.4 %collective-permute-start = (f32[3,4,128,128]{3,2,1,0:T(8,128)}, f32[3,4,128,128]{3,2,1,0:T(8,128)S(1)}, u32[]{:S(2)}, u32[]{:S(2)}) collective-permute-start(f32[3,4,128,128]{3,2,1,0:T(8,128)} %get-tuple-element.519), channel_id=1, source_target_pairs={{0,4},{4,8},{8,12},{12,16},{16,20},{20,24},{24,28},{1,5},{5,9},{9,... | collective-permute-start | bytes 2359304 | tf_op jit(solution)/shard_map/while/body/eval_jaxpr/ppermute | solution.py:16
  120.1 18.6 %collective-permute-start = (f32[3,4,128,128]{3,2,1,0:T(8,128)}, f32[3,4,128,128]{3,2,1,0:T(8,128)S(1)}, u32[]{:S(2)}, u32[]{:S(2)}) collective-permute-start(f32[3,4,128,128]{3,2,1,0:T(8,128)} %get-tuple-element.519), channel_id=1, source_target_pairs={{0,4},{4,8},{8,12},{12,16},{16,20},{20,24},{24,28},{1,5},{5,9},{9,... | collective-permute-start | bytes 2359304 | tf_op jit(solution)/shard_map/while/body/eval_jaxpr/ppermute | solution.py:16
  138.7 17.7 %collective-permute-start = (f32[3,4,128,128]{3,2,1,0:T(8,128)}, f32[3,4,128,128]{3,2,1,0:T(8,128)S(1)}, u32[]{:S(2)}, u32[]{:S(2)}) collective-permute-start(f32[3,4,128,128]{3,2,1,0:T(8,128)} %get-tuple-element.519), channel_id=1, source_target_pairs={{0,4},{4,8},{8,12},{12,16},{16,20},{20,24},{24,28},{1,5},{5,9},{9,... | collective-permute-start | bytes 2359304 | tf_op jit(solution)/shard_map/while/body/eval_jaxpr/ppermute | solution.py:16
  156.4 16.8 %collective-permute-start = (f32[3,4,128,128]{3,2,1,0:T(8,128)}, f32[3,4,128,128]{3,2,1,0:T(8,128)S(1)}, u32[]{:S(2)}, u32[]{:S(2)}) collective-permute-start(f32[3,4,128,128]{3,2,1,0:T(8,128)} %get-tuple-element.519), channel_id=1, source_target_pairs={{0,4},{4,8},{8,12},{12,16},{16,20},{20,24},{24,28},{1,5},{5,9},{9,... | collective-permute-start | bytes 2359304 | tf_op jit(solution)/shard_map/while/body/eval_jaxpr/ppermute | solution.py:16
  173.2 444.4 %collective-permute-start = (f32[3,4,128,128]{3,2,1,0:T(8,128)}, f32[3,4,128,128]{3,2,1,0:T(8,128)S(1)}, u32[]{:S(2)}, u32[]{:S(2)}) collective-permute-start(f32[3,4,128,128]{3,2,1,0:T(8,128)} %get-tuple-element.519), channel_id=1, source_target_pairs={{0,4},{4,8},{8,12},{12,16},{16,20},{20,24},{24,28},{1,5},{5,9},{9,... | collective-permute-start | bytes 2359304 | tf_op jit(solution)/shard_map/while/body/eval_jaxpr/ppermute | solution.py:16
  617.6 2.7 copy-start.6
  617.6 2.7 copy-start.7
  620.3 2.0 copy-start.3
  631.8 3.3 copy-start
  644.9 6.6 copy-start.2
  651.5 1.6 copy-start.1
  651.5 2.8 copy-start.5
  654.3 2.2 copy-start.4
  679.8 16.8 %collective-permute-start = (f32[3,4,128,128]{3,2,1,0:T(8,128)}, f32[3,4,128,128]{3,2,1,0:T(8,128)S(1)}, u32[]{:S(2)}, u32[]{:S(2)}) collective-permute-start(f32[3,4,128,128]{3,2,1,0:T(8,128)} %get-tuple-element.519), channel_id=1, source_target_pairs={{0,4},{4,8},{8,12},{12,16},{16,20},{20,24},{24,28},{1,5},{5,9},{9,... | collective-permute-start | bytes 2359304 | tf_op jit(solution)/shard_map/while/body/eval_jaxpr/ppermute | solution.py:16
  696.6 2.7 copy-start.6
  696.7 2.7 copy-start.7
  699.3 2.0 copy-start.3
  710.8 3.3 copy-start
  723.9 6.6 copy-start.2
  730.5 1.6 copy-start.1
  730.5 2.8 copy-start.5
  733.4 2.2 copy-start.4
where the time goes:
time: 800 us; the launch traced here: 798 us
  waiting for transfers between devices  550 us (69%)
  matrix products  90 us (11%)
  blocking collectives  85.7 us (11%)
  local copies, waits for them, and re-layouts  33.6 us (4%)
  other arithmetic  22.1 us (3%)
  starting transfers between devices  15.1 us (2%)
    ppermute x9, waiting for transfers between devices, passed_along(): return lax.ppermute(value, axis, pairs)  524 us
    psum x9, blocking collectives, one_tick(): totals = lax.psum(jnp.sum(widened * widened, axis=1), 'tok')  55 us
    all_to_all x1, blocking collectives, body(): lax.all_to_all(final_stream, 'tok', split_axis=0, concat_axis=1, tiled=True)  30.7 us
    all_to_all x1, waiting for transfers between devices, body(): lax.all_to_all(tokens, 'tok', split_axis=1, concat_axis=0, tiled=True)  25.6 us
    dot_general x10, matrix products, orthogonalize(): jnp.einsum('...ij,...kj->...ik', current, current, precision=lax.Precisio...  17.7 us
  transfers between devices with their start and end apart: 10, of which 10 were waited for; matrix products, arithmetic and copies ran while one was open for 1% of the time, Pallas kernels for 0%

commit v1 on v0

--- a/solution.py
+++ b/solution.py
@@ -109,7 +109,7 @@
         active = (layer_raw >= 0) & (layer_raw < layer_count)
         layer_now = jnp.clip(layer_raw, 0, layer_count - 1)
         widened = stream.astype(jnp.float32)
-        totals = lax.psum(jnp.sum(widened * widened, axis=1), "tok")
+        totals = jnp.sum(lax.all_gather(jnp.sum(widened * widened, axis=1), "tok"), axis=0)
         inverse = lax.rsqrt(totals / width_all + EPSILON)
         return tick_work(stream, outgoing, layer_now, active, inverse)
 

time: 800 us -> 800 us (level)
    psum x9 -> x0, blocking collectives: 55 us -> none  [one_tick(): totals = lax.psum(jnp.sum(widened * widened, axis=1), 'tok')]
    all_gather x0 -> x9, blocking collectives: none -> 49.9 us  [one_tick(): lax.all_gather(jnp.sum(widened * widened, axis=1), 'tok')]
where the time goes in v1:
time: 800 us; the launch traced here: 799 us
  waiting for transfers between devices  555 us (69%)
  matrix products  90 us (11%)
  blocking collectives  80.5 us (10%)
  local copies, waits for them, and re-layouts  33.7 us (4%)
  other arithmetic  22.2 us (3%)
  starting transfers between devices  15.1 us (2%)
    ppermute x9, waiting for transfers between devices, passed_along(): return lax.ppermute(value, axis, pairs)  530 us
    all_gather x9, blocking collectives, one_tick(): lax.all_gather(jnp.sum(widened * widened, axis=1), 'tok')  49.9 us
    all_to_all x1, blocking collectives, body(): lax.all_to_all(final_stream, 'tok', split_axis=0, concat_axis=1, tiled=True)  30.6 us
    all_to_all x1, waiting for transfers between devices, body(): lax.all_to_all(tokens, 'tok', split_axis=1, concat_axis=0, tiled=True)  25.6 us
    dot_general x10, matrix products, orthogonalize(): jnp.einsum('...ij,...kj->...ik', current, current, precision=lax.Precisio...  17.7 us
  transfers between devices with their start and end apart: 10, of which 10 were waited for; matrix products, arithmetic and copies ran while one was open for 1% of the time, Pallas kernels for 0%

profile of v1, /device:TPU:28, one launch (start us, length us, event | category | flops | bytes accessed | tf_op | source)
XLA Modules:
  0.0 798.9 jit_solution(18080602228949602866)
XLA Ops:
  0.0 3.9 copy.32
  3.9 3.6 all-to-all-start
  7.6 25.6 %all-to-all-done = bf16[512,4,512]{0,2,1:T(8,128)(2,1)S(1)} async-done(((bf16[512,4,512]{0,2,1:T(8,128)(2,1)}), bf16[512,4,512]{0,2,1:T(8,128)(2,1)S(1)}, u32[]{:S(2)}, u32[]{:S(2)}) %all-to-all-start) | async-done | bytes 2097184 | tf_op jit(solution)/shard_map/all_to_all | solution.py:77
  33.2 2.4 copy.33
  35.5 2.9 copy.34
  39.4 720.1 %while.17 = (s32[]{:T(128)}, bf16[2048,512]{0,1:T(8,128)(2,1)S(1)}, f32[3,4,128,128]{3,2,1,0:T(8,128)}, s32[]{:T(128)}, f32[2,5,512]{2,1,0:T(8,128)S(1)}, /*inde...) while((s32[]{:T(128)}, bf16[2048,512]{0,1:T(8,128)(2,1)S(1)}, ...), condition=%wide.region_8.9_spmd, body=%wide.region_0.8_spmd.sunk | while | flops 7005349376 | bytes 224807888 | solution.py:116
  39.4 1.3 collective-permute-start
  41.2 5.2 all-gather.2
  46.4 14.1 %collective-permute-done = f32[3,4,128,128]{3,2,1,0:T(8,128)S(1)} collective-permute-done((f32[3,4,128,128]{3,2,1,0:T(8,128)}, f32[3,4,128,128]{3,2,1,0:T(8,128)S(1)}, u32[]{:S(2)}, u32[]{:S(2)}) %collective-permute-start) | collective-permute-done | bytes 786464 | tf_op jit(solution)/shard_map/while/body/eval_jaxpr/ppermute | solution.py:16
  62.3 5.2 all-gather.2
  67.5 13.3 %collective-permute-done = f32[3,4,128,128]{3,2,1,0:T(8,128)S(1)} collective-permute-done((f32[3,4,128,128]{3,2,1,0:T(8,128)}, f32[3,4,128,128]{3,2,1,0:T(8,128)S(1)}, u32[]{:S(2)}, u32[]{:S(2)}) %collective-permute-start) | collective-permute-done | bytes 786464 | tf_op jit(solution)/shard_map/while/body/eval_jaxpr/ppermute | solution.py:16
  82.5 5.2 all-gather.2
  87.7 13.0 %collective-permute-done = f32[3,4,128,128]{3,2,1,0:T(8,128)S(1)} collective-permute-done((f32[3,4,128,128]{3,2,1,0:T(8,128)}, f32[3,4,128,128]{3,2,1,0:T(8,128)S(1)}, u32[]{:S(2)}, u32[]{:S(2)}) %collective-permute-start) | collective-permute-done | bytes 786464 | tf_op jit(solution)/shard_map/while/body/eval_jaxpr/ppermute | solution.py:16
  102.4 5.2 all-gather.2
  107.6 12.5 %collective-permute-done = f32[3,4,128,128]{3,2,1,0:T(8,128)S(1)} collective-permute-done((f32[3,4,128,128]{3,2,1,0:T(8,128)}, f32[3,4,128,128]{3,2,1,0:T(8,128)S(1)}, u32[]{:S(2)}, u32[]{:S(2)}) %collective-permute-start) | collective-permute-done | bytes 786464 | tf_op jit(solution)/shard_map/while/body/eval_jaxpr/ppermute | solution.py:16
  121.9 5.2 all-gather.2
  127.0 11.6 %collective-permute-done = f32[3,4,128,128]{3,2,1,0:T(8,128)S(1)} collective-permute-done((f32[3,4,128,128]{3,2,1,0:T(8,128)}, f32[3,4,128,128]{3,2,1,0:T(8,128)S(1)}, u32[]{:S(2)}, u32[]{:S(2)}) %collective-permute-start) | collective-permute-done | bytes 786464 | tf_op jit(solution)/shard_map/while/body/eval_jaxpr/ppermute | solution.py:16
  140.4 5.5 all-gather.2
  145.9 10.5 %collective-permute-done = f32[3,4,128,128]{3,2,1,0:T(8,128)S(1)} collective-permute-done((f32[3,4,128,128]{3,2,1,0:T(8,128)}, f32[3,4,128,128]{3,2,1,0:T(8,128)S(1)}, u32[]{:S(2)}, u32[]{:S(2)}) %collective-permute-start) | collective-permute-done | bytes 786464 | tf_op jit(solution)/shard_map/while/body/eval_jaxpr/ppermute | solution.py:16
  158.1 5.8 all-gather.2
  163.9 9.3 %collective-permute-done = f32[3,4,128,128]{3,2,1,0:T(8,128)S(1)} collective-permute-done((f32[3,4,128,128]{3,2,1,0:T(8,128)}, f32[3,4,128,128]{3,2,1,0:T(8,128)S(1)}, u32[]{:S(2)}, u32[]{:S(2)}) %collective-permute-start) | collective-permute-done | bytes 786464 | tf_op jit(solution)/shard_map/while/body/eval_jaxpr/ppermute | solution.py:16
  173.2 1.3 collective-permute-start
  175.0 6.2 all-gather.2
  181.2 437.0 %collective-permute-done = f32[3,4,128,128]{3,2,1,0:T(8,128)S(1)} collective-permute-done((f32[3,4,128,128]{3,2,1,0:T(8,128)}, f32[3,4,128,128]{3,2,1,0:T(8,128)S(1)}, u32[]{:S(2)}, u32[]{:S(2)}) %collective-permute-start) | collective-permute-done | bytes 786464 | tf_op jit(solution)/shard_map/while/body/eval_jaxpr/ppermute | solution.py:16
  618.1 62.3 %conditional.2 = ((bf16[2048,512]{0,1:T(8,128)(2,1)S(1)}, f32[3,4,128,128]{3,2,1,0:T(8,128)})) conditional(s32[]{:T(128)} %convert_element_type.141, (bf16[2048,512]{0,1:T(8,128)(2,1)S(1)}, f32[3,4,128,128]{3,2,1,0:T(8,128)}) %tuple.63, (bf16[2048,512]{0,1:T(8,128)(2,1)S(1)}, s32[]{:T(128)}, f32[2,5,512]{2,1,0:T(8,128)S(1)}, f32[8192]{0:T(1024)S(1)}, ...), branch_computations={%region_2.2_spmd, %region_3.7_spmd} | conditional | flops 7002205696 | bytes 219515520 | solution.py:104
  618.2 2.6 fusion.6
  620.9 1.9 multiply_reduce_fusion.1
  622.9 2.8 fusion.50
  625.7 6.7 fusion.27
  632.4 3.3 fusion.7
  635.7 2.8 fusion.51
  638.5 2.9 fusion.49
  641.4 4.1 copy.28
  645.5 6.6 fusion.35
  654.9 1.6 fusion.38
  657.1 2.4 fusion.41
  659.6 1.9 fusion.44
  663.5 1.7 fusion.61
  667.1 1.7 fusion.62
  670.7 1.7 fusion.63
  674.3 1.8 fusion.64
  682.2 6.5 all-gather.2
  688.7 8.5 %collective-permute-done = f32[3,4,128,128]{3,2,1,0:T(8,128)S(1)} collective-permute-done((f32[3,4,128,128]{3,2,1,0:T(8,128)}, f32[3,4,128,128]{3,2,1,0:T(8,128)S(1)}, u32[]{:S(2)}, u32[]{:S(2)}) %collective-permute-start) | collective-permute-done | bytes 786464 | tf_op jit(solution)/shard_map/while/body/eval_jaxpr/ppermute | solution.py:16
  697.2 62.3 %conditional.2 = ((bf16[2048,512]{0,1:T(8,128)(2,1)S(1)}, f32[3,4,128,128]{3,2,1,0:T(8,128)})) conditional(s32[]{:T(128)} %convert_element_type.141, (bf16[2048,512]{0,1:T(8,128)(2,1)S(1)}, f32[3,4,128,128]{3,2,1,0:T(8,128)}) %tuple.63, (bf16[2048,512]{0,1:T(8,128)(2,1)S(1)}, s32[]{:T(128)}, f32[2,5,512]{2,1,0:T(8,128)S(1)}, f32[8192]{0:T(1024)S(1)}, ...), branch_computations={%region_2.2_spmd, %region_3.7_spmd} | conditional | flops 7002205696 | bytes 219515520 | solution.py:104
  697.3 2.6 fusion.6
  700.0 1.9 multiply_reduce_fusion.1
  702.0 2.8 fusion.50
  704.8 6.7 fusion.27
  711.5 3.3 fusion.7
  714.8 2.8 fusion.51
  717.6 2.9 fusion.49
  720.5 4.1 copy.28
  724.6 6.6 fusion.35
  734.0 1.6 fusion.38
  736.2 2.4 fusion.41
  738.7 1.9 fusion.44
  742.6 1.7 fusion.61
  746.2 1.7 fusion.62
  749.8 1.7 fusion.63
  753.5 1.8 fusion.64
  759.5 2.5 copy.36
  762.0 30.6 %all_to_all.38 = bf16[4,512,512]{2,1,0:T(8,128)(2,1)S(1)} all-to-all(bf16[4,512,512]{2,1,0:T(8,128)(2,1)} %bitcast.167), channel_id=1, replica_groups=mesh['group'=8,'tok'=4] {'tok'}, dimensions={0} | all-to-all | bytes 4194304 | tf_op jit(solution)/shard_map/all_to_all | solution.py:119
  792.6 2.4 copy.37
  795.0 3.9 copy.38
  (111 shorter events, 43.7 us)
Async XLA Ops:
  0.0 7.6 copy-start.9
  3.9 29.2 %all-to-all-start = ((bf16[512,4,512]{0,2,1:T(8,128)(2,1)}), bf16[512,4,512]{0,2,1:T(8,128)(2,1)S(1)}, u32[]{:S(2)}, u32[]{:S(2)}) async-start(bf16[512,4,512]{0,2,1:T(8,128)(2,1)} %bitcast.165), calls=%async_computation | async-start | bytes 4194304 | tf_op jit(solution)/shard_map/all_to_all | solution.py:77
  7.6 31.8 %copy-start.8 = (f32[2,2048]{1,0:T(2,128)S(1)}, f32[2,2048]{1,0:T(2,128)}, u32[]{:S(2)}) copy-start(f32[2,2048]{1,0:T(2,128)} %param.11) | copy-start | bytes 49156
  7.6 31.8 %copy-start.10 = (s32[2,8]{1,0:T(2,128)S(1)}, s32[2,8]{1,0:T(2,128)}, u32[]{:S(2)}) copy-start(s32[2,8]{1,0:T(2,128)} %param.15) | copy-start | bytes 196
  7.6 31.8 %copy-start.11 = (f32[2,4]{1,0:T(2,128)S(1)}, f32[2,4]{1,0:T(2,128)}, u32[]{:S(2)}) copy-start(f32[2,4]{1,0:T(2,128)} %param.14) | copy-start | bytes 100
  39.4 21.1 %collective-permute-start = (f32[3,4,128,128]{3,2,1,0:T(8,128)}, f32[3,4,128,128]{3,2,1,0:T(8,128)S(1)}, u32[]{:S(2)}, u32[]{:S(2)}) collective-permute-start(f32[3,4,128,128]{3,2,1,0:T(8,128)} %get-tuple-element.526), channel_id=1, source_target_pairs={{0,4},{4,8},{8,12},{12,16},{16,20},{20,24},{24,28},{1,5},{5,9},{9,... | collective-permute-start | bytes 2359304 | tf_op jit(solution)/shard_map/while/body/eval_jaxpr/ppermute | solution.py:16
  60.5 20.2 %collective-permute-start = (f32[3,4,128,128]{3,2,1,0:T(8,128)}, f32[3,4,128,128]{3,2,1,0:T(8,128)S(1)}, u32[]{:S(2)}, u32[]{:S(2)}) collective-permute-start(f32[3,4,128,128]{3,2,1,0:T(8,128)} %get-tuple-element.526), channel_id=1, source_target_pairs={{0,4},{4,8},{8,12},{12,16},{16,20},{20,24},{24,28},{1,5},{5,9},{9,... | collective-permute-start | bytes 2359304 | tf_op jit(solution)/shard_map/while/body/eval_jaxpr/ppermute | solution.py:16
  80.8 19.9 %collective-permute-start = (f32[3,4,128,128]{3,2,1,0:T(8,128)}, f32[3,4,128,128]{3,2,1,0:T(8,128)S(1)}, u32[]{:S(2)}, u32[]{:S(2)}) collective-permute-start(f32[3,4,128,128]{3,2,1,0:T(8,128)} %get-tuple-element.526), channel_id=1, source_target_pairs={{0,4},{4,8},{8,12},{12,16},{16,20},{20,24},{24,28},{1,5},{5,9},{9,... | collective-permute-start | bytes 2359304 | tf_op jit(solution)/shard_map/while/body/eval_jaxpr/ppermute | solution.py:16
  100.7 19.4 %collective-permute-start = (f32[3,4,128,128]{3,2,1,0:T(8,128)}, f32[3,4,128,128]{3,2,1,0:T(8,128)S(1)}, u32[]{:S(2)}, u32[]{:S(2)}) collective-permute-start(f32[3,4,128,128]{3,2,1,0:T(8,128)} %get-tuple-element.526), channel_id=1, source_target_pairs={{0,4},{4,8},{8,12},{12,16},{16,20},{20,24},{24,28},{1,5},{5,9},{9,... | collective-permute-start | bytes 2359304 | tf_op jit(solution)/shard_map/while/body/eval_jaxpr/ppermute | solution.py:16
  120.1 18.6 %collective-permute-start = (f32[3,4,128,128]{3,2,1,0:T(8,128)}, f32[3,4,128,128]{3,2,1,0:T(8,128)S(1)}, u32[]{:S(2)}, u32[]{:S(2)}) collective-permute-start(f32[3,4,128,128]{3,2,1,0:T(8,128)} %get-tuple-element.526), channel_id=1, source_target_pairs={{0,4},{4,8},{8,12},{12,16},{16,20},{20,24},{24,28},{1,5},{5,9},{9,... | collective-permute-start | bytes 2359304 | tf_op jit(solution)/shard_map/while/body/eval_jaxpr/ppermute | solution.py:16
  138.7 17.7 %collective-permute-start = (f32[3,4,128,128]{3,2,1,0:T(8,128)}, f32[3,4,128,128]{3,2,1,0:T(8,128)S(1)}, u32[]{:S(2)}, u32[]{:S(2)}) collective-permute-start(f32[3,4,128,128]{3,2,1,0:T(8,128)} %get-tuple-element.526), channel_id=1, source_target_pairs={{0,4},{4,8},{8,12},{12,16},{16,20},{20,24},{24,28},{1,5},{5,9},{9,... | collective-permute-start | bytes 2359304 | tf_op jit(solution)/shard_map/while/body/eval_jaxpr/ppermute | solution.py:16
  156.4 16.8 %collective-permute-start = (f32[3,4,128,128]{3,2,1,0:T(8,128)}, f32[3,4,128,128]{3,2,1,0:T(8,128)S(1)}, u32[]{:S(2)}, u32[]{:S(2)}) collective-permute-start(f32[3,4,128,128]{3,2,1,0:T(8,128)} %get-tuple-element.526), channel_id=1, source_target_pairs={{0,4},{4,8},{8,12},{12,16},{16,20},{20,24},{24,28},{1,5},{5,9},{9,... | collective-permute-start | bytes 2359304 | tf_op jit(solution)/shard_map/while/body/eval_jaxpr/ppermute | solution.py:16
  173.2 444.9 %collective-permute-start = (f32[3,4,128,128]{3,2,1,0:T(8,128)}, f32[3,4,128,128]{3,2,1,0:T(8,128)S(1)}, u32[]{:S(2)}, u32[]{:S(2)}) collective-permute-start(f32[3,4,128,128]{3,2,1,0:T(8,128)} %get-tuple-element.526), channel_id=1, source_target_pairs={{0,4},{4,8},{8,12},{12,16},{16,20},{20,24},{24,28},{1,5},{5,9},{9,... | collective-permute-start | bytes 2359304 | tf_op jit(solution)/shard_map/while/body/eval_jaxpr/ppermute | solution.py:16
  618.1 2.7 copy-start.6
  618.2 2.7 copy-start.7
  620.9 2.0 copy-start.3
  632.4 3.3 copy-start
  645.5 6.6 copy-start.2
  652.1 1.6 copy-start.1
  652.1 2.8 copy-start.5
  654.9 2.2 copy-start.4
  680.4 16.8 %collective-permute-start = (f32[3,4,128,128]{3,2,1,0:T(8,128)}, f32[3,4,128,128]{3,2,1,0:T(8,128)S(1)}, u32[]{:S(2)}, u32[]{:S(2)}) collective-permute-start(f32[3,4,128,128]{3,2,1,0:T(8,128)} %get-tuple-element.526), channel_id=1, source_target_pairs={{0,4},{4,8},{8,12},{12,16},{16,20},{20,24},{24,28},{1,5},{5,9},{9,... | collective-permute-start | bytes 2359304 | tf_op jit(solution)/shard_map/while/body/eval_jaxpr/ppermute | solution.py:16
  697.2 2.7 copy-start.6
  697.3 2.7 copy-start.7
  700.0 2.0 copy-start.3
  711.5 3.3 copy-start
  724.6 6.6 copy-start.2
  731.2 1.6 copy-start.1
  731.2 2.8 copy-start.5
  734.0 2.2 copy-start.4
